TPU v7x, 32 devices: a whole 2x2x4 slice. The times are simulated.
32 devices in a mesh: group: 4 (over y, x), depth: 2 (over core), mp: 4 (over z).
Axes of the slice: x: 2, y: 2, z: 4, core: 2. Of those that a mesh axis runs over, the one named last changes fastest.
Arguments:
- states: bfloat16 [64, 4096], P(('group', 'depth', 'mp')), may hold values from -6 to 6
- queries: bfloat16 [64, 32, 128], P('group', 'mp'), may hold values from -6 to 6
- new_keys: bfloat16 [64, 8, 128], P('group', 'mp'), may hold values from -18 to 18
- new_values: bfloat16 [64, 8, 128], P('group', 'mp'), may hold values from -24 to 24
- text_keys: bfloat16 [64, 8, 512, 128], P('group', 'mp', 'depth'), may hold values from -6 to 6
- text_values: bfloat16 [64, 8, 512, 128], P('group', 'mp', 'depth'), may hold values from -24 to 24
- text_length: int32 [64], P('group'), may hold values from 2 to 512
- image_keys: bfloat16 [32, 8, 576, 128], P('group', 'mp'), may hold values from -6 to 6
- image_values: bfloat16 [32, 8, 576, 128], P('group', 'mp'), may hold values from -24 to 24
- image_slot: int32 [32], replicated, may hold values from 0 to 31, as said below
- block_list: int32 [4, 32], replicated, may hold values from 0 to 31, as said below
- block_count: int32 [4], replicated, may hold values from 16 to 32, as said below
- image_first: int32 [64], P('group'), may hold values from 0 to 31, as said below
- image_count: int32 [64], P('group'), may hold values from 1 to 2
- out_weight: bfloat16 [4096, 4096], P('mp'), may hold values from -0.09375 to 0.09375
- norm_gain: float32 [4096], replicated, may hold values from 0.5 to 1.5
- gate_weight: bfloat16 [4096, 14336], P(None, ('group', 'mp')), may hold values from -0.09375 to 0.09375
- up_weight: bfloat16 [4096, 14336], P(None, ('group', 'mp')), may hold values from -0.09375 to 0.09375
- down_weight: bfloat16 [14336, 4096], P(('group', 'mp')), may hold values from -0.046875 to 0.046875
Outputs:
- attention: bfloat16 [64, 32, 128], P(('group', 'depth'), 'mp')
- layer_out: bfloat16 [64, 4096], P(('group', 'depth', 'mp'))
Inputs may be any that keep to these rules, and one draw needn't show every extreme that they name: `image_slot`: a permutation. The owner group of hash k is image_slot[k] // 8. `block_list`: the hashes of one group's list are distinct. Among one group's places with the same remainder modulo 2, at most 4 belongs to any one owner group; some group has block_count 32, and there every owner group holds exactly 4 place of every remainder. `block_count`: the sum of image_count over the group's requests. The requests of a group take consecutive list places in request order: image_first is the sum of image_count over the group's earlier requests.
All inputs are finite; a program needn't handle non-finite values.
Results may differ from a plain program's by a relative error of at most 0.012.
Values may be sent and summed in bfloat16 or wider, within the bound.
A program may use at most 128 MiB of HBM per device.

v0:
```python
import functools
import math

import jax
import jax.numpy as jnp
from jax import lax
from jax.experimental import pallas as pl
from jax.experimental.pallas import tpu as pltpu
from jax.sharding import PartitionSpec as P

LOG_TWO = math.log(2.0)
MASKED_SCORE = -1e30
NORM_EPSILON = 1e-05
READS = 2
MESH = pl.DeviceIdType.MESH
F32 = jnp.float32
BF16 = jnp.bfloat16
NT = (((1,), (1,)), ((), ()))


def tile_of(size, most):
    for tile in (most, most // 2, most // 4):
        if size % tile == 0:
            return tile
    return size


def kernel(
    dims,
    states,
    queries,
    new_keys,
    new_values,
    norm_gain,
    text_length,
    image_slot,
    block_list,
    block_count,
    image_first,
    image_count,
    text_keys_hbm,
    text_values_hbm,
    image_keys_hbm,
    image_values_hbm,
    out_weight_hbm,
    gate_hbm,
    up_hbm,
    down_hbm,
    attention_out,
    layer_out,
    text_keys,
    text_values,
    image_keys,
    image_values,
    out_weight,
    gate,
    up,
    down,
    chosen,
    codes,
    readers,
    query_send,
    query_recv,
    text_scores,
    new_scores,
    text_weights,
    text_part,
    text_recv,
    image_scores,
    image_weights,
    image_send,
    stat_send,
    image_recv,
    stat_recv,
    merged,
    flat,
    projected,
    proj_send,
    proj_recv,
    residual,
    norm_all,
    tokens,
    tokens_low,
    gate_sum,
    up_sum,
    hidden,
    down_sum,
    down_send,
    down_recv,
    load_sem,
    query_ssem,
    query_rsem,
    text_ssem,
    text_rsem,
    image_ssem,
    image_rsem,
    stat_ssem,
    stat_rsem,
    proj_ssem,
    proj_rsem,
    norm_ssem,
    norm_rsem,
    down_ssem,
    down_rsem,
):
    groups, depths, mps = dims
    pieces = groups * mps
    g = lax.axis_index("group")
    d = lax.axis_index("depth")
    m = lax.axis_index("mp")
    me = g * mps + m
    requests, heads, width = queries.shape
    kv_heads, span = text_keys.shape[1], text_keys.shape[2]
    share = heads // kv_heads
    stored, patches = image_keys.shape[0], image_keys.shape[2]
    listed = block_list.shape[1]
    steps = listed // depths
    copies = listed // (depths * groups)
    per_depth = requests // depths
    rows = states.shape[0]
    model = states.shape[1]
    scaling = 1.0 / math.sqrt(width)

    pairs = (
        (text_keys_hbm, text_keys),
        (text_values_hbm, text_values),
        (image_keys_hbm, image_keys),
        (image_values_hbm, image_values),
        (out_weight_hbm, out_weight),
        (gate_hbm, gate),
        (up_hbm, up),
        (down_hbm, down),
    )
    loads = [pltpu.make_async_copy(a, b, load_sem.at[i]) for i, (a, b) in enumerate(pairs)]
    for load in loads[:4]:
        load.start()

    barrier = pltpu.get_barrier_semaphore()

    def greet_piece(k, carry):
        peer = lax.rem(me + k, pieces)
        pl.semaphore_signal(
            barrier, inc=1, device_id=(peer // mps, d, lax.rem(peer, mps)), device_id_type=MESH
        )
        return carry

    lax.fori_loop(1, pieces, greet_piece, 0)
    for e in range(1, depths):

        def greet_depth(k, carry):
            pl.semaphore_signal(
                barrier,
                inc=1,
                device_id=(lax.rem(g + k, groups), lax.rem(d + e, depths), m),
                device_id_type=MESH,
            )
            return carry

        lax.fori_loop(0, groups, greet_depth, 0)

    own_count = block_count[g]

    def place_step(i, counts):
        out = []
        for p in range(depths):
            place = i * depths + p
            owner = image_slot[block_list[g, place]] // stored
            rank = jnp.int32(0)
            for o in range(groups):
                rank = jnp.where(owner == o, counts[p * groups + o], rank)
            codes[place] = jnp.minimum(owner * copies + rank, groups * copies - 1)
            live = (place < own_count).astype(jnp.int32)
            for o in range(groups):
                out.append(counts[p * groups + o] + jnp.where(owner == o, live, 0))
        return tuple(out)

    lax.fori_loop(0, steps, place_step, (jnp.int32(0),) * (depths * groups))

    def reader_step(r, found):
        for k in range(READS):
            place = image_first[r] + k
            held = jnp.minimum(place, listed - 1)
            good = (k < image_count[r]) & (place < own_count) & (lax.rem(place, depths) == d)
            code = jnp.where(good, codes[held], -1)
            found = tuple(jnp.where(code == i, r, old) for i, old in enumerate(found))
        return found

    found = lax.fori_loop(0, requests, reader_step, (jnp.int32(0),) * (groups * copies))
    for i, reader in enumerate(found):
        readers[i] = reader
    for o in range(groups):
        for c in range(copies):
            query_send[o, c] = queries[readers[o * copies + c]]
    query_recv[g] = query_send[g]

    pl.semaphore_wait(barrier, pieces - 1 + (depths - 1) * groups)

    def query_copy(peer, slot):
        return pltpu.make_async_remote_copy(
            src_ref=query_send.at[peer],
            dst_ref=query_recv.at[slot],
            send_sem=query_ssem.at[peer],
            recv_sem=query_rsem.at[slot],
            device_id=(peer, d, m),
            device_id_type=MESH,
        )

    def over(count, action):
        def body(k, carry):
            action(k)
            return carry

        lax.fori_loop(1, count, body, 0, unroll=True)

    over(groups, lambda k: query_copy(lax.rem(g + k, groups), g).start())

    def serve_step(i, state):
        place = i * depths + d
        out = []
        for s in range(groups):
            rank, picked = state[s]
            slot = image_slot[block_list[s, place]]
            hit = ((slot // stored) == g) & (place < block_count[s])
            within = lax.rem(slot, stored)
            target = jnp.where(hit, rank, -1)
            picked = tuple(jnp.where(target == c, within, old) for c, old in enumerate(picked))
            out.append((rank + hit.astype(jnp.int32), picked))
        return tuple(out)

    zero = jnp.int32(0)
    served = lax.fori_loop(0, steps, serve_step, ((zero, (zero,) * copies),) * groups)
    for s in range(groups):
        for c in range(copies):
            chosen[s * copies + c] = served[s][1][c]

    def by_head(parts):
        result = parts[0]
        row = lax.broadcasted_iota(jnp.int32, result.shape, 0)
        for h in range(1, kv_heads):
            result = jnp.where(row >= h * share, parts[h], result)
        return result

    def spread_rows(small):
        return by_head(
            [jnp.broadcast_to(small[h : h + 1, :], (heads, width)) for h in range(kv_heads)]
        )

    loads[0].wait()
    loads[4].start()
    lanes = lax.broadcasted_iota(jnp.int32, (heads, span), 1) + d * span

    def text_first(r, carry):
        q = queries[r]
        score = by_head(
            [
                lax.dot_general(q, text_keys[r, h], NT, preferred_element_type=F32)
                for h in range(kv_heads)
            ]
        )
        text_scores[r] = jnp.where(lanes < text_length[r], score * scaling, MASKED_SCORE)
        key = spread_rows(new_keys[r].astype(F32))
        new_score = jnp.sum(q.astype(F32) * key, axis=-1, keepdims=True) * scaling
        new_scores[r] = jnp.broadcast_to(new_score, (heads, width))
        return carry

    lax.fori_loop(0, requests, text_first, 0, unroll=4)
    is_first = jnp.full((requests, heads, width), d, jnp.int32) == 0
    score = text_scores[...]
    fresh = jnp.where(is_first, new_scores[...], MASKED_SCORE)
    top = jnp.maximum(jnp.max(score, axis=-1, keepdims=True), fresh)
    level = jnp.floor(top / LOG_TWO)
    text_part[:, 1] = level
    weight = jnp.where(
        score > 0.5 * MASKED_SCORE, jnp.exp(score - LOG_TWO * level[:, :, :1]), 0.0
    ).astype(BF16)
    text_weights[...] = weight
    fresh_weight = jnp.where(is_first, jnp.exp(new_scores[...] - LOG_TWO * level), 0.0)
    fresh_weight = fresh_weight.astype(BF16).astype(F32)
    new_scores[...] = fresh_weight
    text_part[:, 2] = jnp.sum(weight.astype(F32), axis=-1, keepdims=True) + fresh_weight
    loads[1].wait()

    def text_second(r, carry):
        w = text_weights[r]
        value = by_head(
            [
                jnp.dot(w, text_values[r, h], preferred_element_type=F32)
                for h in range(kv_heads)
            ]
        )
        text_part[r, 0] = value + new_scores[r] * spread_rows(new_values[r].astype(F32))
        return carry

    lax.fori_loop(0, requests, text_second, 0, unroll=4)

    def text_copy(peer, slot):
        return pltpu.make_async_remote_copy(
            src_ref=text_part.at[pl.ds(peer * per_depth, per_depth)],
            dst_ref=text_recv.at[slot],
            send_sem=text_ssem.at[peer],
            recv_sem=text_rsem.at[slot],
            device_id=(g, peer, m),
            device_id_type=MESH,
        )

    over(depths, lambda k: text_copy(lax.rem(d + k, depths), d).start())
    for load in loads[5:]:
        load.start()

    loads[2].wait()
    loads[3].wait()

    stat_lane = lax.broadcasted_iota(jnp.int32, (heads, width), 1)

    def serve(s):
        slots = [chosen[s * copies + c] for c in range(copies)]
        for c in range(copies):
            q = query_recv[s, c]
            image_scores[c] = scaling * by_head(
                [
                    lax.dot_general(q, image_keys[slots[c], h], NT, preferred_element_type=F32)
                    for h in range(kv_heads)
                ]
            )
        score = image_scores[...]
        level = jnp.floor(jnp.max(score, axis=-1, keepdims=True) / LOG_TWO)
        weight = jnp.exp(score - LOG_TWO * level).astype(BF16)
        image_weights[...] = weight
        total = jnp.sum(weight.astype(F32), axis=-1, keepdims=True)
        stats = jnp.zeros((heads, width), F32)
        for c in range(copies):
            stats = jnp.where(stat_lane == 2 * c, level[c], stats)
            stats = jnp.where(stat_lane == 2 * c + 1, total[c], stats)
        stat_send[s] = stats
        for c in range(copies):
            w = image_weights[c]
            image_send[s, c] = by_head(
                [
                    jnp.dot(w, image_values[slots[c], h], preferred_element_type=F32)
                    for h in range(kv_heads)
                ]
            ).astype(BF16)

    def image_copy(peer, depth, slot, slot_depth):
        return pltpu.make_async_remote_copy(
            src_ref=image_send.at[peer],
            dst_ref=image_recv.at[slot_depth, pl.ds(slot * copies, copies)],
            send_sem=image_ssem.at[depth, peer],
            recv_sem=image_rsem.at[slot_depth, slot],
            device_id=(peer, depth, m),
            device_id_type=MESH,
        )

    def stat_copy(peer, depth, slot, slot_depth):
        return pltpu.make_async_remote_copy(
            src_ref=stat_send.at[peer],
            dst_ref=stat_recv.at[slot_depth, slot],
            send_sem=stat_ssem.at[depth, peer],
            recv_sem=stat_rsem.at[slot_depth, slot],
            device_id=(peer, depth, m),
            device_id_type=MESH,
        )

    serve(g)
    stat_recv[d, g] = stat_send[g]
    image_recv[d, pl.ds(g * copies, copies)] = image_send[g]
    for e in range(1, depths):
        image_copy(g, lax.rem(d + e, depths), g, d).start()
        stat_copy(g, lax.rem(d + e, depths), g, d).start()

    def serve_other(k):
        s = lax.rem(g + k, groups)
        query_copy(s, s).wait_recv()
        serve(s)
        for e in range(depths):
            image_copy(s, lax.rem(d + e, depths), g, d).start()
            stat_copy(s, lax.rem(d + e, depths), g, d).start()

    over(groups, serve_other)

    over(depths, lambda k: text_copy(lax.rem(d + k, depths), lax.rem(d + k, depths)).wait_recv())
    for e in range(1, depths):
        other = lax.rem(d + e, depths)
        image_copy(g, other, g, other).wait_recv()
        stat_copy(g, other, g, other).wait_recv()

    def image_arrival(k):
        s = lax.rem(g + k, groups)
        for e in range(depths):
            other = lax.rem(d + e, depths)
            image_copy(s, other, s, other).wait_recv()
            stat_copy(s, other, s, other).wait_recv()

    over(groups, image_arrival)
    text_recv[d] = text_part[pl.ds(d * per_depth, per_depth)]

    def stat_of(stats, lane):
        picked = jnp.sum(jnp.where(stat_lane == lane, stats, 0.0), axis=-1, keepdims=True)
        return jnp.broadcast_to(picked, (heads, width))

    def merge(i, carry):
        r = d * per_depth + i
        parts = [tuple(text_recv[e, i, n] for n in range(3)) for e in range(depths)]
        for k in range(READS):
            place = image_first[r] + k
            good = (k < image_count[r]) & (place < own_count)
            held = jnp.minimum(place, listed - 1)
            code = codes[held]
            at = lax.rem(held, depths)
            stats = stat_recv[at, code // copies]
            rank = lax.rem(code, copies)
            live = jnp.full((heads, width), good.astype(jnp.int32), jnp.int32) == 1
            parts.append(
                (
                    jnp.where(live, image_recv[at, code].astype(F32), 0.0),
                    jnp.where(live, stat_of(stats, 2 * rank), MASKED_SCORE),
                    jnp.where(live, stat_of(stats, 2 * rank + 1), 0.0),
                )
            )
        highest = functools.reduce(jnp.maximum, [part[1] for part in parts])
        factors = [jnp.exp2(part[1] - highest) for part in parts]
        total = sum(part[2] * factor for part, factor in zip(parts, factors))
        value = sum(part[0] * factor for part, factor in zip(parts, factors)) / total
        merged[i] = value
        attention_out[i] = value.astype(BF16)
        return carry

    lax.fori_loop(0, per_depth, merge, 0, unroll=2)
    for h in range(heads):
        flat[:, h * width : (h + 1) * width] = merged[:, h, :]

    loads[4].wait()
    low = flat[...].astype(BF16)
    tile = tile_of(model, 512)

    def project(n, carry):
        columns = pl.ds(pl.multiple_of(n * tile, tile), tile)
        projected[:, columns] = jnp.dot(low, out_weight[:, columns], preferred_element_type=F32)
        return carry

    lax.fori_loop(0, model // tile, project, 0)
    for i in range(mps):
        proj_send[i] = projected[i * rows : (i + 1) * rows, :].astype(proj_send.dtype)

    def proj_copy(peer, slot):
        return pltpu.make_async_remote_copy(
            src_ref=proj_send.at[peer],
            dst_ref=proj_recv.at[slot],
            send_sem=proj_ssem.at[peer],
            recv_sem=proj_rsem.at[slot],
            device_id=(g, d, peer),
            device_id_type=MESH,
        )

    over(mps, lambda k: proj_copy(lax.rem(m + k, mps), m).start())
    proj_recv[m] = proj_send[m]
    over(mps, lambda k: proj_copy(lax.rem(m + k, mps), lax.rem(m + k, mps)).wait_recv())
    total = states[...].astype(F32)
    for i in range(mps):
        total = total + proj_recv[i].astype(F32)
    residual[...] = total
    spread = jnp.mean(total * total, axis=-1, keepdims=True)
    norm_all[me] = (total * lax.rsqrt(spread + NORM_EPSILON) * norm_gain[...]).astype(BF16)

    def norm_copy(peer, slot):
        return pltpu.make_async_remote_copy(
            src_ref=norm_all.at[me],
            dst_ref=norm_all.at[slot],
            send_sem=norm_ssem.at[peer],
            recv_sem=norm_rsem.at[slot],
            device_id=(peer // mps, d, lax.rem(peer, mps)),
            device_id_type=MESH,
        )

    over(pieces, lambda k: norm_copy(lax.rem(me + k, pieces), me).start())
    loads[5].wait()
    loads[6].wait()
    loads[7].wait()
    over(pieces, lambda k: norm_copy(lax.rem(me + k, pieces), lax.rem(me + k, pieces)).wait_recv())
    for i in range(pieces):
        tokens[i * rows : (i + 1) * rows, :] = norm_all[i].astype(F32)
    tokens_low[...] = tokens[...].astype(BF16)
    gate_sum[...] = jnp.zeros_like(gate_sum)
    up_sum[...] = jnp.zeros_like(up_sum)

    def expand(k, carry):
        part = pl.ds(pl.multiple_of(k * tile, tile), tile)
        x = tokens_low[:, part]
        gate_sum[...] += jnp.dot(x, gate[part, :], preferred_element_type=F32)
        up_sum[...] += jnp.dot(x, up[part, :], preferred_element_type=F32)
        return carry

    lax.fori_loop(0, model // tile, expand, 0)
    v = gate_sum[...]
    hidden[...] = (v / (1.0 + jnp.exp(-v)) * up_sum[...]).astype(BF16)

    def contract(n, carry):
        columns = pl.ds(pl.multiple_of(n * tile, tile), tile)
        down_sum[:, columns] = jnp.dot(hidden[...], down[:, columns], preferred_element_type=F32)
        return carry

    lax.fori_loop(0, model // tile, contract, 0)
    for i in range(pieces):
        down_send[i] = down_sum[i * rows : (i + 1) * rows, :].astype(down_send.dtype)

    def down_copy(peer, slot):
        return pltpu.make_async_remote_copy(
            src_ref=down_send.at[peer],
            dst_ref=down_recv.at[slot],
            send_sem=down_ssem.at[peer],
            recv_sem=down_rsem.at[slot],
            device_id=(peer // mps, d, lax.rem(peer, mps)),
            device_id_type=MESH,
        )

    over(pieces, lambda k: down_copy(lax.rem(me + k, pieces), me).start())
    down_recv[me] = down_send[me]
    over(pieces, lambda k: down_copy(lax.rem(me + k, pieces), lax.rem(me + k, pieces)).wait_recv())

    def add_piece(i, total):
        return total + down_recv[i].astype(F32)

    layer_out[...] = lax.fori_loop(0, pieces, add_piece, residual[...]).astype(BF16)

    over(groups, lambda k: query_copy(lax.rem(g + k, groups), g).wait_send())
    over(depths, lambda k: text_copy(lax.rem(d + k, depths), d).wait_send())
    for e in range(1, depths):
        image_copy(g, lax.rem(d + e, depths), g, d).wait_send()
        stat_copy(g, lax.rem(d + e, depths), g, d).wait_send()

    def image_gone(k):
        for e in range(depths):
            image_copy(lax.rem(g + k, groups), lax.rem(d + e, depths), g, d).wait_send()
            stat_copy(lax.rem(g + k, groups), lax.rem(d + e, depths), g, d).wait_send()

    over(groups, image_gone)
    over(mps, lambda k: proj_copy(lax.rem(m + k, mps), m).wait_send())
    over(pieces, lambda k: norm_copy(lax.rem(me + k, pieces), me).wait_send())
    over(pieces, lambda k: down_copy(lax.rem(me + k, pieces), me).wait_send())


def on_device(
    states,
    queries,
    new_keys,
    new_values,
    text_keys,
    text_values,
    text_length,
    image_keys,
    image_values,
    image_slot,
    block_list,
    block_count,
    image_first,
    image_count,
    out_weight,
    norm_gain,
    gate_weight,
    up_weight,
    down_weight,
):
    groups = lax.axis_size("group")
    depths = lax.axis_size("depth")
    mps = lax.axis_size("mp")
    pieces = groups * mps
    requests, heads, width = queries.shape
    listed = block_list.shape[1]
    copies = listed // (depths * groups)
    per_depth = requests // depths
    rows, model = states.shape
    units = gate_weight.shape[1]
    span = text_keys.shape[2]
    patches = image_keys.shape[2]
    dma = pltpu.SemaphoreType.DMA
    vmem = pl.BlockSpec(memory_space=pltpu.VMEM)
    smem = pl.BlockSpec(memory_space=pltpu.SMEM)
    hbm = pl.BlockSpec(memory_space=pl.ANY)
    big = (
        text_keys,
        text_values,
        image_keys,
        image_values,
        out_weight,
        gate_weight,
        up_weight,
        down_weight,
    )
    scratch = [pltpu.VMEM(a.shape, a.dtype) for a in big]
    scratch += [
        pltpu.SMEM((groups * copies,), jnp.int32),
        pltpu.SMEM((listed,), jnp.int32),
        pltpu.SMEM((groups * copies,), jnp.int32),
        pltpu.VMEM((groups, copies, heads, width), BF16),
        pltpu.VMEM((groups, copies, heads, width), BF16),
        pltpu.VMEM((requests, heads, span), F32),
        pltpu.VMEM((requests, heads, width), F32),
        pltpu.VMEM((requests, heads, span), BF16),
        pltpu.VMEM((requests, 3, heads, width), F32),
        pltpu.VMEM((depths, per_depth, 3, heads, width), F32),
        pltpu.VMEM((copies, heads, patches), F32),
        pltpu.VMEM((copies, heads, patches), BF16),
        pltpu.VMEM((groups, copies, heads, width), BF16),
        pltpu.VMEM((groups, heads, width), F32),
        pltpu.VMEM((depths, groups * copies, heads, width), BF16),
        pltpu.VMEM((depths, groups, heads, width), F32),
        pltpu.VMEM((per_depth, heads, width), F32),
        pltpu.VMEM((per_depth, heads * width), F32),
        pltpu.VMEM((per_depth, model), F32),
        pltpu.VMEM((mps, rows, model), BF16),
        pltpu.VMEM((mps, rows, model), BF16),
        pltpu.VMEM((rows, model), F32),
        pltpu.VMEM((pieces, rows, model), BF16),
        pltpu.VMEM((pieces * rows, model), F32),
        pltpu.VMEM((pieces * rows, model), BF16),
        pltpu.VMEM((pieces * rows, units), F32),
        pltpu.VMEM((pieces * rows, units), F32),
        pltpu.VMEM((pieces * rows, units), BF16),
        pltpu.VMEM((pieces * rows, model), F32),
        pltpu.VMEM((pieces, rows, model), BF16),
        pltpu.VMEM((pieces, rows, model), BF16),
        dma((len(big),)),
        dma((groups,)),
        dma((groups,)),
        dma((depths,)),
        dma((depths,)),
        dma((depths, groups)),
        dma((depths, groups)),
        dma((depths, groups)),
        dma((depths, groups)),
        dma((mps,)),
        dma((mps,)),
        dma((pieces,)),
        dma((pieces,)),
        dma((pieces,)),
        dma((pieces,)),
    ]
    return pl.pallas_call(
        functools.partial(kernel, (groups, depths, mps)),
        out_shape=(
            jax.ShapeDtypeStruct((per_depth, heads, width), BF16),
            jax.ShapeDtypeStruct((rows, model), BF16),
        ),
        in_specs=[vmem] * 5 + [smem] * 6 + [hbm] * 8,
        out_specs=(vmem, vmem),
        scratch_shapes=scratch,
        compiler_params=pltpu.CompilerParams(
            collective_id=0, has_side_effects=True, vmem_limit_bytes=67043328
        ),
    )(
        states,
        queries,
        new_keys,
        new_values,
        norm_gain.reshape(1, model),
        text_length,
        image_slot,
        block_list,
        block_count,
        image_first,
        image_count,
        *big,
    )


def solution(mesh):
    placed = (
        P(("group", "depth", "mp"), None),
        P("group", "mp", None),
        P("group", "mp", None),
        P("group", "mp", None),
        P("group", "mp", "depth", None),
        P("group", "mp", "depth", None),
        P("group"),
        P("group", "mp", None, None),
        P("group", "mp", None, None),
        P(),
        P(),
        P(),
        P("group"),
        P("group"),
        P("mp", None),
        P(),
        P(None, ("group", "mp")),
        P(None, ("group", "mp")),
        P(("group", "mp"), None),
    )
    return jax.shard_map(
        on_device,
        mesh=mesh,
        in_specs=placed,
        out_specs=(P(("group", "depth"), "mp", None), P(("group", "depth", "mp"), None)),
        check_vma=False,
    )
```

profile of v0, /device:TPU:0, one launch (start us, length us, event | category | flops | bytes accessed | tf_op | source)
XLA Modules:
  0.0 46.0 jit_solution(9792282836442375942)
XLA Ops:
  0.6 42.7 %shard_map.194 = (bf16[8,8,128]{2,1,0:T(8,128)(2,1)}, bf16[2,4096]{1,0:T(2,128)(2,1)}) custom-call(bf16[2,4096]{1,0:T(2,128)(2,1)} %states.1, bf16[16,8,128]{2,1,0:T(8,128)(2,1)} %queries.1, bf16[16,2,128]{2,1,0:T(2,128)(2,1)} %new_keys.1, bf16[16,2,128]{2,1,0:T(2,128)(2,1)} %new_values.1, f32[1,4096]{1,0:T(1,128)} %bitcast.1, s32[16]{0:T(128)} %text_length.1, ...), custom_call_target="tpu_custom_call" | custom-call | tf_op jit(solution)/shard_map/pallas_call | solution.py:638
  43.3 1.3 %copy.23 = bf16[8,8,128]{2,1,0:T(8,128)(2,1)} copy(bf16[8,8,128]{2,1,0:T(8,128)(2,1)} %get-tuple-element.4) | data formatting | bytes 32768
  44.7 1.3 %copy.24 = bf16[2,4096]{1,0:T(2,128)(2,1)} copy(bf16[2,4096]{1,0:T(2,128)(2,1)} %get-tuple-element.5) | data formatting | bytes 32768
where the time goes:
time: 46.4 us; the launch traced here: 46 us
  Pallas kernels  42.7 us (92%)
  local copies, waits for them, and re-layouts  2.66 us (6%)
  between operations  0.65 us (1%)
    pallas_call x1, Pallas kernels, on_device(): pl.pallas_call(functools.partial(kernel, (groups, depths, mps)), out_shap...  42.7 us
    unnamed x2, local copies, waits for them, and re-layouts  2.66 us

commit v1 on v0

v1 whole, which is shorter than its diff:
```python
import functools
import math

import jax
import jax.numpy as jnp
from jax import lax
from jax.experimental import pallas as pl
from jax.experimental.pallas import tpu as pltpu
from jax.sharding import PartitionSpec as P

LOG_TWO = math.log(2.0)
MASKED_SCORE = -1e30
NORM_EPSILON = 1e-05
READS = 2
DOWN_CHUNKS = 2
MESH = pl.DeviceIdType.MESH
F32 = jnp.float32
BF16 = jnp.bfloat16
I32 = jnp.int32
NT = (((1,), (1,)), ((), ()))


def kernel(
    dims,
    states_hbm,
    queries_hbm,
    new_keys_hbm,
    new_values_hbm,
    gain_hbm,
    text_length_hbm,
    image_slot_hbm,
    block_list_hbm,
    block_count_hbm,
    image_first_hbm,
    image_count_hbm,
    text_keys_hbm,
    text_values_hbm,
    image_keys_hbm,
    image_values_hbm,
    out_weight_hbm,
    gate_hbm,
    up_hbm,
    down_hbm,
    attention_out,
    layer_out,
    queries,
    new_keys,
    new_values,
    gain,
    text_length,
    image_slot,
    block_list,
    block_count,
    image_first,
    image_count,
    text_keys,
    text_values,
    image_keys,
    image_values,
    out_weight,
    gate,
    up,
    down,
    chosen,
    codes,
    states_recv,
    query_send,
    query_recv,
    text_scores,
    new_scores,
    text_weights,
    text_part,
    text_recv,
    image_send,
    stat_send,
    image_recv,
    stat_recv,
    merged,
    flat,
    proj_send,
    proj_recv,
    states_rows,
    res_cols,
    res_send,
    res_recv,
    x_all,
    square_all,
    gate_sum,
    up_sum,
    hidden,
    down_send,
    down_recv,
    load_sem,
    small_sem,
    state_ssem,
    state_rsem,
    query_ssem,
    query_rsem,
    text_ssem,
    text_rsem,
    image_ssem,
    image_rsem,
    stat_ssem,
    stat_rsem,
    proj_ssem,
    proj_rsem,
    x_ssem,
    x_rsem,
    square_ssem,
    square_rsem,
    res_ssem,
    res_rsem,
    down_ssem,
    down_rsem,
    ready_sem,
):
    groups, depths, mps = dims
    pieces = groups * mps
    g = lax.axis_index("group")
    d = lax.axis_index("depth")
    m = lax.axis_index("mp")
    requests, heads, width = queries.shape
    kv_heads, span = text_keys.shape[1], text_keys.shape[2]
    share = heads // kv_heads
    stored, patches = image_keys.shape[0], image_keys.shape[2]
    listed = block_list.shape[1]
    steps = listed // depths
    copies = listed // (depths * groups)
    places = groups * copies
    per_depth = requests // depths
    rows = states_recv.shape[1]
    model = layer_out.shape[1]
    cols = model // mps
    chunks, part_cols = down_recv.shape[1], down_recv.shape[3]
    scaling = 1.0 / math.sqrt(width)
    far = [(m + k) % mps for k in range(1, mps)]
    if mps % 2 == 0:
        half = m // (mps // 2)
        far = [
            (1 - half) * (mps - 1 - k - (m + k) // (mps - 1)) + half * (k + (mps - 1 + k - m) // (mps - 1))
            for k in range(mps - 1)
        ]
    near = list(reversed(far))
    plane = [(g + k) % groups for k in range(1, groups)]

    barrier = pltpu.get_barrier_semaphore()

    def tell(sem, gg, dd, mm):
        pl.semaphore_signal(sem, inc=1, device_id=(gg, dd, mm), device_id_type=MESH)

    for peer in far:
        tell(barrier, g, d, peer)
    for peer in plane:
        tell(barrier, peer, d, m)
    for e in range(1, depths):
        for k in range(groups):
            tell(barrier, (g + k) % groups, (d + e) % depths, m)

    own_columns = pl.ds(pl.multiple_of(m * cols, cols), cols)
    small_pairs = (
        (image_slot_hbm, image_slot),
        (block_list_hbm, block_list),
        (block_count_hbm, block_count),
        (image_first_hbm, image_first),
        (image_count_hbm, image_count),
        (text_length_hbm, text_length),
        (queries_hbm, queries),
        (new_keys_hbm, new_keys),
        (new_values_hbm, new_values),
        (gain_hbm.at[:, own_columns], gain),
        (states_hbm.at[:, own_columns], states_recv.at[m]),
    )
    smalls = [pltpu.make_async_copy(a, b, small_sem.at[i]) for i, (a, b) in enumerate(small_pairs)]
    for small in smalls:
        small.start()
    pairs = (
        (text_keys_hbm, text_keys),
        (text_values_hbm, text_values),
        (image_keys_hbm, image_keys),
        (image_values_hbm, image_values),
        (out_weight_hbm, out_weight),
        (gate_hbm, gate),
        (up_hbm, up),
        (down_hbm, down),
    )
    loads = [pltpu.make_async_copy(a, b, load_sem.at[i]) for i, (a, b) in enumerate(pairs)]
    for load in loads[:4]:
        load.start()

    def remote(src, dst, ssem, rsem, gg, dd, mm):
        return pltpu.make_async_remote_copy(
            src_ref=src,
            dst_ref=dst,
            send_sem=ssem,
            recv_sem=rsem,
            device_id=(gg, dd, mm),
            device_id_type=MESH,
        )

    for small in smalls[:6]:
        small.wait()

    own_count = block_count[g]
    counts = [jnp.int32(0)] * (depths * groups)
    for place in range(listed):
        p = place % depths
        owner = lax.div(image_slot[block_list[g, place]], jnp.int32(stored))
        live = (place < own_count).astype(I32)
        rank = jnp.int32(0)
        for o in range(groups):
            mine = owner == o
            rank = jnp.where(mine, counts[p * groups + o], rank)
            counts[p * groups + o] = counts[p * groups + o] + jnp.where(mine, live, 0)
        codes[place] = jnp.minimum(owner * copies + rank, places - 1)

    def wanted(r):
        found = jnp.int32(-1)
        for k in range(READS):
            place = image_first[r] + k
            held = jnp.minimum(place, listed - 1)
            good = (k < image_count[r]) & (place < own_count) & (lax.rem(place, depths) == d)
            found = jnp.where(good, codes[held], found)
        return found

    smalls[6].wait()
    picked = [jnp.zeros((heads, width), F32)] * places
    for r in range(requests):
        code = jnp.full((heads, width), wanted(r), I32)
        q = queries[r].astype(F32)
        picked = [jnp.where(code == i, q, old) for i, old in enumerate(picked)]
    for o in range(groups):
        for c in range(copies):
            query_send[o, c] = picked[o * copies + c].astype(BF16)
    query_recv[g] = query_send[g]

    pl.semaphore_wait(barrier, groups - 1 + (depths - 1) * groups + mps - 1)

    def query_copy(peer, slot):
        return remote(
            query_send.at[peer], query_recv.at[slot], query_ssem, query_rsem.at[slot], peer, d, m
        )

    for peer in plane:
        query_copy(peer, g).start()
    for peer in far:
        tell(ready_sem, g, d, peer)

    def state_copy(peer):
        columns = pl.ds(pl.multiple_of(peer * cols, cols), cols)
        return remote(
            states_hbm.at[:, columns], states_recv.at[m], state_ssem, state_rsem, g, d, peer
        )

    for peer in far:
        state_copy(peer).start()

    def serve_step(i, state):
        place = i * depths + d
        out = []
        for s in range(groups):
            rank, held = state[s]
            slot = image_slot[block_list[s, place]]
            hit = (lax.div(slot, jnp.int32(stored)) == g) & (place < block_count[s])
            within = lax.rem(slot, jnp.int32(stored))
            target = jnp.where(hit, rank, -1)
            held = tuple(jnp.where(target == c, within, old) for c, old in enumerate(held))
            out.append((rank + hit.astype(I32), held))
        return tuple(out)

    zero = jnp.int32(0)
    served = lax.fori_loop(0, steps, serve_step, ((zero, (zero,) * copies),) * groups, unroll=2)
    for s in range(groups):
        for c in range(copies):
            chosen[s * copies + c] = served[s][1][c]

    def by_head(parts):
        result = parts[0]
        row = lax.broadcasted_iota(I32, result.shape, 0)
        for h in range(1, kv_heads):
            result = jnp.where(row >= h * share, parts[h], result)
        return result

    def spread_rows(small):
        return by_head(
            [jnp.broadcast_to(small[h : h + 1, :], (heads, width)) for h in range(kv_heads)]
        )

    def widen(q):
        full = q.astype(F32)
        row = lax.broadcasted_iota(I32, full.shape, 0)
        parts = [
            jnp.where((row >= h * share) & (row < (h + 1) * share), full, 0.0)
            for h in range(kv_heads)
        ]
        return jnp.concatenate(parts, axis=1).astype(BF16)

    def joined(ref, index):
        return jnp.concatenate([ref[index, h] for h in range(kv_heads)], axis=1)

    def split_heads(wide):
        return by_head([wide[:, h * width : (h + 1) * width] for h in range(kv_heads)])

    smalls[7].wait()
    smalls[8].wait()
    loads[0].wait()
    loads[4].start()
    lanes = lax.broadcasted_iota(I32, (heads, span), 1) + d * span

    def text_first(r, carry):
        q = queries[r]
        score = lax.dot_general(widen(q), joined(text_keys, r), NT, preferred_element_type=F32)
        text_scores[r] = jnp.where(lanes < text_length[r], score * scaling, MASKED_SCORE)
        key = spread_rows(new_keys[r].astype(F32))
        new_score = jnp.sum(q.astype(F32) * key, axis=-1, keepdims=True) * scaling
        new_scores[r] = jnp.broadcast_to(new_score, (heads, width))
        return carry

    lax.fori_loop(0, requests, text_first, 0, unroll=4)
    is_first = jnp.full((requests, heads, width), d, I32) == 0
    score = text_scores[...]
    fresh = jnp.where(is_first, new_scores[...], MASKED_SCORE)
    top = jnp.maximum(jnp.max(score, axis=-1, keepdims=True), fresh)
    level = jnp.floor(top / LOG_TWO)
    text_part[:, 1] = level
    weight = jnp.where(
        score > 0.5 * MASKED_SCORE, jnp.exp(score - LOG_TWO * level[:, :, :1]), 0.0
    ).astype(BF16)
    text_weights[...] = weight
    fresh_weight = jnp.where(is_first, jnp.exp(new_scores[...] - LOG_TWO * level), 0.0)
    fresh_weight = fresh_weight.astype(BF16).astype(F32)
    new_scores[...] = fresh_weight
    text_part[:, 2] = jnp.sum(weight.astype(F32), axis=-1, keepdims=True) + fresh_weight
    loads[1].wait()

    def text_second(r, carry):
        wide = jnp.dot(text_weights[r], joined(text_values, r), preferred_element_type=F32)
        fresh_value = new_scores[r] * spread_rows(new_values[r].astype(F32))
        text_part[r, 0] = split_heads(wide) + fresh_value
        return carry

    lax.fori_loop(0, requests, text_second, 0, unroll=4)

    def text_copy(peer, slot):
        return remote(
            text_part.at[pl.ds(peer * per_depth, per_depth)],
            text_recv.at[slot],
            text_ssem,
            text_rsem.at[slot],
            g,
            peer,
            m,
        )

    others = [(d + e) % depths for e in range(1, depths)]
    for other in others:
        text_copy(other, d).start()
    for load in loads[5:]:
        load.start()
    text_recv[d] = text_part[pl.ds(d * per_depth, per_depth)]

    loads[2].wait()
    loads[3].wait()
    stat_lane = lax.broadcasted_iota(I32, (heads, width), 1)
    stat_row = lax.broadcasted_iota(I32, (heads, width), 0)
    own_lane = lax.rem(stat_lane, heads) == stat_row
    stat_kind = lax.div(stat_lane, heads)

    def serve(s):
        slots = [chosen[s * copies + c] for c in range(copies)]
        scores = [
            scaling
            * lax.dot_general(
                widen(query_recv[s, c]),
                joined(image_keys, slots[c]),
                NT,
                preferred_element_type=F32,
            )
            for c in range(copies)
        ]
        stats = jnp.zeros((heads, width), F32)
        weights = []
        for c in range(copies):
            level = jnp.floor(jnp.max(scores[c], axis=-1, keepdims=True) / LOG_TWO)
            weight = jnp.exp(scores[c] - LOG_TWO * level).astype(BF16)
            total = jnp.sum(weight.astype(F32), axis=-1, keepdims=True)
            stats = jnp.where(stat_kind == 2 * c, level, stats)
            stats = jnp.where(stat_kind == 2 * c + 1, total, stats)
            weights.append(weight)
        stat_send[s] = jnp.sum(jnp.where(own_lane, stats, 0.0), axis=0, keepdims=True)
        for c in range(copies):
            wide = jnp.dot(weights[c], joined(image_values, slots[c]), preferred_element_type=F32)
            image_send[s, c] = split_heads(wide).astype(BF16)

    def image_copy(peer, depth):
        return remote(
            image_send.at[peer],
            image_recv.at[pl.ds((d * groups + g) * copies, copies)],
            image_ssem,
            image_rsem,
            peer,
            depth,
            m,
        )

    def stat_copy(peer, depth):
        return remote(
            stat_send.at[peer],
            stat_recv.at[d * groups + g],
            stat_ssem,
            stat_rsem,
            peer,
            depth,
            m,
        )

    serve(g)
    stat_recv[d * groups + g] = stat_send[g]
    image_recv[pl.ds((d * groups + g) * copies, copies)] = image_send[g]
    for other in others:
        image_copy(g, other).start()
        stat_copy(g, other).start()

    def serve_other(k, carry):
        s = lax.rem(g + k, groups)
        query_copy(s, s).wait_recv()
        serve(s)
        for e in range(depths):
            image_copy(s, lax.rem(d + e, depths)).start()
            stat_copy(s, lax.rem(d + e, depths)).start()
        return carry

    lax.fori_loop(1, groups, serve_other, 0, unroll=True)

    remote(states_recv.at[pl.ds(0, mps - 1)], states_recv.at[pl.ds(0, mps - 1)], state_ssem, state_rsem, g, d, m).wait_recv()
    smalls[9].wait()
    smalls[10].wait()
    for i in range(mps):
        states_rows[i * rows : (i + 1) * rows, :] = states_recv[i].astype(F32)

    for other in others:
        text_copy(other, other).wait_recv()
    arrivals = depths * groups - 1
    image_all = image_recv.at[pl.ds(0, arrivals * copies)]
    stat_all = stat_recv.at[pl.ds(0, arrivals)]
    remote(stat_all, stat_all, stat_ssem, stat_rsem, g, d, m).wait_recv()
    remote(image_all, image_all, image_ssem, image_rsem, g, d, m).wait_recv()

    def stat_of(stats, lane):
        picked = jnp.sum(jnp.where(stat_lane == lane + stat_row, stats, 0.0), axis=-1, keepdims=True)
        return jnp.broadcast_to(picked, (heads, width))

    def merge(i, carry):
        r = d * per_depth + i
        parts = [tuple(text_recv[e, i, n] for n in range(3)) for e in range(depths)]
        for k in range(READS):
            place = image_first[r] + k
            good = (k < image_count[r]) & (place < own_count)
            held = jnp.minimum(place, listed - 1)
            code = codes[held]
            at = lax.rem(held, depths)
            owner = lax.div(code, jnp.int32(copies))
            rank = lax.rem(code, jnp.int32(copies))
            stats = jnp.broadcast_to(stat_recv[at * groups + owner], (heads, width))
            live = jnp.full((heads, width), good.astype(I32), I32) == 1
            parts.append(
                (
                    jnp.where(live, image_recv[at * places + code].astype(F32), 0.0),
                    jnp.where(live, stat_of(stats, 2 * rank * heads), MASKED_SCORE),
                    jnp.where(live, stat_of(stats, (2 * rank + 1) * heads), 0.0),
                )
            )
        highest = functools.reduce(jnp.maximum, [part[1] for part in parts])
        factors = [jnp.exp2(part[1] - highest) for part in parts]
        total = sum(part[2] * factor for part, factor in zip(parts, factors))
        value = sum(part[0] * factor for part, factor in zip(parts, factors)) / total
        merged[i] = value
        attention_out[i] = value.astype(BF16)
        return carry

    lax.fori_loop(0, per_depth, merge, 0, unroll=True)
    for h in range(heads):
        flat[:, h * width : (h + 1) * width] = merged[:, h, :]

    loads[4].wait()
    low = flat[...].astype(BF16)

    def project(block):
        columns = pl.ds(pl.multiple_of(block * cols, cols), cols)
        return jnp.dot(low, out_weight[:, columns], preferred_element_type=F32)

    def proj_copy(k, peer):
        return remote(proj_send.at[k], proj_recv.at[m], proj_ssem, proj_rsem, g, d, peer)

    for k, peer in enumerate(far):
        proj_send[k] = project(peer).astype(BF16)
        proj_copy(k, peer).start()
    total = project(m) + states_rows[...]
    sent = proj_send.at[pl.ds(0, mps - 1)]
    remote(sent, proj_recv.at[pl.ds(0, mps - 1)], proj_ssem, proj_rsem, g, d, m).wait_recv()
    for k in range(1, mps):
        total = total + proj_recv[lax.rem(m + k, mps)].astype(F32)
    res_cols[...] = total
    me = m * groups + g
    x_all[me] = (total * gain[...]).astype(BF16)
    square = jnp.broadcast_to(jnp.sum(total * total, axis=-1, keepdims=True), (per_depth, width))
    square_lane = lax.broadcasted_iota(I32, (per_depth, width), 1)
    square_row = lax.broadcasted_iota(I32, (per_depth, width), 0)
    diagonal = square_lane == square_row
    square_all[me] = jnp.sum(jnp.where(diagonal, square, 0.0), axis=0, keepdims=True)

    pl.semaphore_wait(ready_sem, mps - 1)

    def x_copy(gg, mm):
        return remote(x_all.at[me], x_all.at[me], x_ssem, x_rsem.at[m], gg, d, mm)

    def square_copy(gg, mm):
        return remote(square_all.at[me], square_all.at[me], square_ssem, square_rsem, gg, d, mm)

    targets = [(peer, m) for peer in plane]
    for block in far:
        targets += [((g + k) % groups, block) for k in range(groups)]
    for gg, mm in targets:
        x_copy(gg, mm).start()
    for gg, mm in targets:
        square_copy(gg, mm).start()

    for i in range(mps):
        res_send[i] = res_cols[i * rows : (i + 1) * rows, :]

    def res_copy(peer):
        return remote(res_send.at[peer], res_recv.at[m], res_ssem, res_rsem, g, d, peer)

    for peer in far:
        res_copy(peer).start()
    res_recv[m] = res_send[m]

    loads[5].wait()
    loads[6].wait()
    loads[7].wait()

    def expand(block, first):
        tokens = [x_all[block * groups + s].astype(F32) for s in range(groups)]
        tokens = jnp.concatenate(tokens, axis=0).astype(BF16)
        part = pl.ds(pl.multiple_of(block * cols, cols), cols)
        a = jnp.dot(tokens, gate[part, :], preferred_element_type=F32)
        b = jnp.dot(tokens, up[part, :], preferred_element_type=F32)
        if first:
            gate_sum[...] = a
            up_sum[...] = b
        else:
            gate_sum[...] += a
            up_sum[...] += b

    def x_wait(block, count):
        got = x_all.at[pl.ds(0, count)]
        remote(got, got, x_ssem, x_rsem.at[block], g, d, m).wait_recv()

    x_wait(m, groups - 1)
    expand(m, True)
    for i, block in enumerate([lax.rem(m + k, mps) for k in range(1, mps)]):
        if i == mps - 2:
            got = square_all.at[pl.ds(0, pieces - 1)]
            remote(got, got, square_ssem, square_rsem, g, d, m).wait_recv()
            scales = []
            for s in range(groups):
                row = sum(square_all[i2 * groups + s] for i2 in range(mps))
                row = jnp.broadcast_to(row, (per_depth, width))
                mean = jnp.sum(jnp.where(diagonal, row, 0.0), axis=-1, keepdims=True) / model
                scales.append(lax.rsqrt(mean + NORM_EPSILON))
            scale = jnp.concatenate(scales, axis=0)
        x_wait(block, groups)
        expand(block, False)
    v = gate_sum[...] * scale
    hidden[...] = (v / (1.0 + jnp.exp(-v)) * (up_sum[...] * scale)).astype(BF16)

    def down_copy(n, gg, mm):
        return remote(
            down_send.at[n, mm * groups + gg],
            down_recv.at[me, n],
            down_ssem,
            down_rsem,
            gg,
            d,
            mm,
        )

    order = targets[groups - 1 :] + targets[: groups - 1]
    for n in range(chunks):
        columns = slice(n * part_cols, (n + 1) * part_cols)
        part = jnp.dot(hidden[...], down[:, columns], preferred_element_type=F32)
        for s in range(groups):
            for i in range(mps):
                at = s * per_depth + i * rows
                down_send[n, i * groups + s] = part[at : at + rows, :].astype(BF16)
        for gg, mm in order:
            down_copy(n, gg, mm).start()
    down_recv[me] = down_send[:, me]

    got = res_recv.at[pl.ds(0, mps - 1)]
    remote(got, got, res_ssem, res_rsem, g, d, m).wait_recv()
    got = down_recv.at[pl.ds(0, pieces - 1)]
    remote(got, got, down_ssem, down_rsem, g, d, m).wait_recv()

    for n in range(chunks):

        def add_piece(i, total):
            return total + down_recv[i, n].astype(F32)

        summed = lax.fori_loop(0, pieces, add_piece, jnp.zeros((rows, part_cols), F32), unroll=4)
        for i in range(mps):
            low_edge, high_edge = max(n * part_cols, i * cols), min((n + 1) * part_cols, (i + 1) * cols)
            if low_edge < high_edge:
                layer_out[:, low_edge:high_edge] = (
                    summed[:, low_edge - n * part_cols : high_edge - n * part_cols]
                    + res_recv[i, :, low_edge - i * cols : high_edge - i * cols]
                ).astype(BF16)

    def sent_all(ref, ssem, rsem):
        remote(ref, ref, ssem, rsem, g, d, m).wait_send()

    sent_all(states_recv.at[pl.ds(0, mps - 1)], state_ssem, state_rsem)
    sent_all(query_send.at[pl.ds(0, groups - 1)], query_ssem, query_rsem.at[0])
    for other in others:
        text_copy(other, d).wait_send()
    sent_all(image_all, image_ssem, image_rsem)
    sent_all(stat_all, stat_ssem, stat_rsem)
    sent_all(proj_send.at[pl.ds(0, mps - 1)], proj_ssem, proj_rsem)
    sent_all(x_all.at[pl.ds(0, pieces - 1)], x_ssem, x_rsem.at[0])
    sent_all(square_all.at[pl.ds(0, pieces - 1)], square_ssem, square_rsem)
    sent_all(res_send.at[pl.ds(0, mps - 1)], res_ssem, res_rsem)
    sent_all(down_recv.at[pl.ds(0, pieces - 1)], down_ssem, down_rsem)


def finish(attention, layer, attention_out, layer_out):
    attention_out[...] = attention[...]
    layer_out[...] = layer[...]


def on_device(
    states,
    queries,
    new_keys,
    new_values,
    text_keys,
    text_values,
    text_length,
    image_keys,
    image_values,
    image_slot,
    block_list,
    block_count,
    image_first,
    image_count,
    out_weight,
    norm_gain,
    gate_weight,
    up_weight,
    down_weight,
):
    groups = lax.axis_size("group")
    depths = lax.axis_size("depth")
    mps = lax.axis_size("mp")
    pieces = groups * mps
    requests, heads, width = queries.shape
    listed = block_list.shape[1]
    copies = listed // (depths * groups)
    per_depth = requests // depths
    rows, model = states.shape
    cols = model // mps
    units = gate_weight.shape[1]
    span = text_keys.shape[2]
    part_cols = model // DOWN_CHUNKS
    dma = pltpu.SemaphoreType.DMA
    vmem = pl.BlockSpec(memory_space=pltpu.VMEM)
    hbm = pl.BlockSpec(memory_space=pl.ANY)
    small = (
        states,
        queries,
        new_keys,
        new_values,
        norm_gain.reshape(1, model),
        text_length,
        image_slot,
        block_list,
        block_count,
        image_first,
        image_count,
    )
    big = (
        text_keys,
        text_values,
        image_keys,
        image_values,
        out_weight,
        gate_weight,
        up_weight,
        down_weight,
    )
    scratch = [pltpu.VMEM(a.shape, a.dtype) for a in small[1:4]]
    scratch += [pltpu.VMEM((1, cols), norm_gain.dtype)]
    scratch += [pltpu.SMEM(a.shape, a.dtype) for a in small[5:]]
    scratch += [pltpu.VMEM(a.shape, a.dtype) for a in big]
    scratch += [
        pltpu.SMEM((groups * copies,), I32),
        pltpu.SMEM((listed,), I32),
        pltpu.VMEM((mps, rows, cols), BF16),
        pltpu.VMEM((groups, copies, heads, width), BF16),
        pltpu.VMEM((groups, copies, heads, width), BF16),
        pltpu.VMEM((requests, heads, span), F32),
        pltpu.VMEM((requests, heads, width), F32),
        pltpu.VMEM((requests, heads, span), BF16),
        pltpu.VMEM((requests, 3, heads, width), F32),
        pltpu.VMEM((depths, per_depth, 3, heads, width), F32),
        pltpu.VMEM((groups, copies, heads, width), BF16),
        pltpu.VMEM((groups, 1, width), F32),
        pltpu.VMEM((depths * groups * copies, heads, width), BF16),
        pltpu.VMEM((depths * groups, 1, width), F32),
        pltpu.VMEM((per_depth, heads, width), F32),
        pltpu.VMEM((per_depth, heads * width), F32),
        pltpu.VMEM((mps, per_depth, cols), BF16),
        pltpu.VMEM((mps, per_depth, cols), BF16),
        pltpu.VMEM((per_depth, cols), F32),
        pltpu.VMEM((per_depth, cols), F32),
        pltpu.VMEM((mps, rows, cols), F32),
        pltpu.VMEM((mps, rows, cols), F32),
        pltpu.VMEM((pieces, per_depth, cols), BF16),
        pltpu.VMEM((pieces, 1, width), F32),
        pltpu.VMEM((groups * per_depth, units), F32),
        pltpu.VMEM((groups * per_depth, units), F32),
        pltpu.VMEM((groups * per_depth, units), BF16),
        pltpu.VMEM((DOWN_CHUNKS, pieces, rows, part_cols), BF16),
        pltpu.VMEM((pieces, DOWN_CHUNKS, rows, part_cols), BF16),
        dma((len(big),)),
        dma((len(small),)),
        dma,
        dma,
        dma,
        dma((groups,)),
        dma,
        dma((depths,)),
        dma,
        dma,
        dma,
        dma,
        dma,
        dma,
        dma,
        dma((mps,)),
        dma,
        dma,
        dma,
        dma,
        dma,
        dma,
        pltpu.SemaphoreType.REGULAR,
    ]
    raw = pl.pallas_call(
        functools.partial(kernel, (groups, depths, mps)),
        out_shape=(
            pltpu.VMEM((per_depth, heads, width), BF16),
            pltpu.VMEM((rows, model), BF16),
        ),
        in_specs=[hbm] * 19,
        out_specs=(vmem, vmem),
        scratch_shapes=scratch,
        compiler_params=pltpu.CompilerParams(
            collective_id=0, has_side_effects=True, vmem_limit_bytes=60000000
        ),
    )(*small, *big)
    return pl.pallas_call(
        finish,
        out_shape=(
            jax.ShapeDtypeStruct((per_depth, heads, width), BF16),
            jax.ShapeDtypeStruct((rows, model), BF16),
        ),
        in_specs=[vmem] * 2,
        out_specs=(vmem, vmem),
    )(*(pltpu.with_memory_space_constraint(r, pltpu.VMEM) for r in raw))


def solution(mesh):
    placed = (
        P(("group", "depth", "mp"), None),
        P("group", "mp", None),
        P("group", "mp", None),
        P("group", "mp", None),
        P("group", "mp", "depth", None),
        P("group", "mp", "depth", None),
        P("group"),
        P("group", "mp", None, None),
        P("group", "mp", None, None),
        P(),
        P(),
        P(),
        P("group"),
        P("group"),
        P("mp", None),
        P(),
        P(None, ("group", "mp")),
        P(None, ("group", "mp")),
        P(("group", "mp"), None),
    )
    return jax.shard_map(
        on_device,
        mesh=mesh,
        in_specs=placed,
        out_specs=(P(("group", "depth"), "mp", None), P(("group", "depth", "mp"), None)),
        check_vma=False,
    )
```

time: 46.4 us -> 37.5 us (0.81)
  Pallas kernels: 42.7 us -> 36.7 us
  local copies, waits for them, and re-layouts: 2.66 us -> 0 us
    pallas_call x1, Pallas kernels: 42.7 us -> 36.1 us  [on_device(): pl.pallas_call(functools.partial(kernel, (groups, depths, mps)), out_shap...]
    unnamed x2 -> x0, local copies, waits for them, and re-layouts: 2.66 us -> none
    pallas_call x0 -> x1, Pallas kernels: none -> 0.61 us  [on_device(): pl.pallas_call(finish, out_shape=(jax.ShapeDtypeStruct((per_depth, heads,...]
where the time goes in v1:
time: 37.5 us; the launch traced here: 37.3 us
  Pallas kernels  36.7 us (98%)
  between operations  0.65 us (2%)
    pallas_call x1, Pallas kernels, on_device(): pl.pallas_call(functools.partial(kernel, (groups, depths, mps)), out_shap...  36.1 us

profile of v1, /device:TPU:0, one launch (start us, length us, event | category | flops | bytes accessed | tf_op | source)
XLA Modules:
  0.0 37.3 jit_solution(12501479562221128319)
XLA Ops:
  0.6 36.1 %shard_map.194 = (bf16[8,8,128]{2,1,0:T(8,128)(2,1)S(1)}, bf16[2,4096]{1,0:T(2,128)(2,1)S(1)}) custom-call(bf16[2,4096]{1,0:T(2,128)(2,1)} %states_hbm.1, bf16[16,8,128]{2,1,0:T(8,128)(2,1)} %queries_hbm.1, bf16[16,2,128]{2,1,0:T(2,128)(2,1)} %new_keys_hbm.1, bf16[16,2,128]{2,1,0:T(2,128)(2,1)} %new_values_hbm.1, f32[1,4096]{1,0:T(1,128)} %bitcast.1, ...), custom_call_target="tpu_custom_call" | custom-call | tf_op jit(solution)/shard_map/pallas_call | solution.py:757
  36.7 0.6 %shard_map.195 = (bf16[8,8,128]{2,1,0:T(8,128)(2,1)}, bf16[2,4096]{1,0:T(2,128)(2,1)}) custom-call(bf16[8,8,128]{2,1,0:T(8,128)(2,1)S(1)} %get-tuple-element.4.attention, bf16[2,4096]{1,0:T(2,128)(2,1)S(1)} %get-tuple-element.5.layer), custom_call_target="tpu_custom_call" | custom-call | tf_op jit(solution)/shard_map/pallas_call | solution.py:770

commit v2 on v1

--- a/solution.py
+++ b/solution.py
@@ -12,7 +12,7 @@
 MASKED_SCORE = -1e30
 NORM_EPSILON = 1e-05
 READS = 2
-DOWN_CHUNKS = 2
+DOWN_CHUNKS = 1
 MESH = pl.DeviceIdType.MESH
 F32 = jnp.float32
 BF16 = jnp.bfloat16
@@ -84,6 +84,7 @@
     res_send,
     res_recv,
     x_all,
+    square_cols,
     square_all,
     gate_sum,
     up_sum,
@@ -106,6 +107,7 @@
     proj_rsem,
     x_ssem,
     x_rsem,
+    hand_rsem,
     square_ssem,
     square_rsem,
     res_ssem,
@@ -133,15 +135,22 @@
     cols = model // mps
     chunks, part_cols = down_recv.shape[1], down_recv.shape[3]
     scaling = 1.0 / math.sqrt(width)
-    far = [(m + k) % mps for k in range(1, mps)]
+    far = [lax.rem(m + k, mps) for k in range(1, mps)]
     if mps % 2 == 0:
-        half = m // (mps // 2)
+        half = lax.div(m, mps // 2)
         far = [
-            (1 - half) * (mps - 1 - k - (m + k) // (mps - 1)) + half * (k + (mps - 1 + k - m) // (mps - 1))
+            (1 - half) * (mps - 1 - k - lax.div(m + k, mps - 1))
+            + half * (k + lax.div(mps - 1 + k - m, mps - 1))
             for k in range(mps - 1)
         ]
-    near = list(reversed(far))
-    plane = [(g + k) % groups for k in range(1, groups)]
+    near = [lax.rem(m + k, mps) for k in range(1, mps) if k != mps // 2]
+    if mps == 4:
+        near = [m + 1 - 2 * lax.rem(m, 2), 3 - m]
+    plane = [lax.rem(g + k, groups) for k in range(1, groups)]
+    serving = plane
+    if groups == 4:
+        beside = g + 1 - 2 * lax.rem(g, 2)
+        serving = [beside, lax.rem(beside + 2, groups), lax.rem(g + 2, groups)]
 
     barrier = pltpu.get_barrier_semaphore()
 
@@ -154,7 +163,7 @@
         tell(barrier, peer, d, m)
     for e in range(1, depths):
         for k in range(groups):
-            tell(barrier, (g + k) % groups, (d + e) % depths, m)
+            tell(barrier, lax.rem(g + k, groups), lax.rem(d + e, depths), m)
 
     own_columns = pl.ds(pl.multiple_of(m * cols, cols), cols)
     small_pairs = (
@@ -184,8 +193,8 @@
         (down_hbm, down),
     )
     loads = [pltpu.make_async_copy(a, b, load_sem.at[i]) for i, (a, b) in enumerate(pairs)]
-    for load in loads[:4]:
-        load.start()
+    for i in (0, 2, 3, 1):
+        loads[i].start()
 
     def remote(src, dst, ssem, rsem, gg, dd, mm):
         return pltpu.make_async_remote_copy(
@@ -303,7 +312,6 @@
     smalls[7].wait()
     smalls[8].wait()
     loads[0].wait()
-    loads[4].start()
     lanes = lax.broadcasted_iota(I32, (heads, span), 1) + d * span
 
     def text_first(r, carry):
@@ -315,7 +323,7 @@
         new_scores[r] = jnp.broadcast_to(new_score, (heads, width))
         return carry
 
-    lax.fori_loop(0, requests, text_first, 0, unroll=4)
+    lax.fori_loop(0, requests, text_first, 0, unroll=True)
     is_first = jnp.full((requests, heads, width), d, I32) == 0
     score = text_scores[...]
     fresh = jnp.where(is_first, new_scores[...], MASKED_SCORE)
@@ -330,36 +338,11 @@
     fresh_weight = fresh_weight.astype(BF16).astype(F32)
     new_scores[...] = fresh_weight
     text_part[:, 2] = jnp.sum(weight.astype(F32), axis=-1, keepdims=True) + fresh_weight
-    loads[1].wait()
-
-    def text_second(r, carry):
-        wide = jnp.dot(text_weights[r], joined(text_values, r), preferred_element_type=F32)
-        fresh_value = new_scores[r] * spread_rows(new_values[r].astype(F32))
-        text_part[r, 0] = split_heads(wide) + fresh_value
-        return carry
-
-    lax.fori_loop(0, requests, text_second, 0, unroll=4)
-
-    def text_copy(peer, slot):
-        return remote(
-            text_part.at[pl.ds(peer * per_depth, per_depth)],
-            text_recv.at[slot],
-            text_ssem,
-            text_rsem.at[slot],
-            g,
-            peer,
-            m,
-        )
-
-    others = [(d + e) % depths for e in range(1, depths)]
-    for other in others:
-        text_copy(other, d).start()
-    for load in loads[5:]:
-        load.start()
-    text_recv[d] = text_part[pl.ds(d * per_depth, per_depth)]
-
+    others = [lax.rem(d + e, depths) for e in range(1, depths)]
     loads[2].wait()
     loads[3].wait()
+    for load in loads[4:]:
+        load.start()
     stat_lane = lax.broadcasted_iota(I32, (heads, width), 1)
     stat_row = lax.broadcasted_iota(I32, (heads, width), 0)
     own_lane = lax.rem(stat_lane, heads) == stat_row
@@ -420,16 +403,37 @@
         image_copy(g, other).start()
         stat_copy(g, other).start()
 
-    def serve_other(k, carry):
-        s = lax.rem(g + k, groups)
+    loads[1].wait()
+
+    def text_second(r, carry):
+        wide = jnp.dot(text_weights[r], joined(text_values, r), preferred_element_type=F32)
+        fresh_value = new_scores[r] * spread_rows(new_values[r].astype(F32))
+        text_part[r, 0] = split_heads(wide) + fresh_value
+        return carry
+
+    lax.fori_loop(0, requests, text_second, 0, unroll=True)
+
+    def text_copy(peer, slot):
+        return remote(
+            text_part.at[pl.ds(peer * per_depth, per_depth)],
+            text_recv.at[slot],
+            text_ssem,
+            text_rsem.at[slot],
+            g,
+            peer,
+            m,
+        )
+
+    for other in others:
+        text_copy(other, d).start()
+    text_recv[d] = text_part[pl.ds(d * per_depth, per_depth)]
+
+    for s in serving:
         query_copy(s, s).wait_recv()
         serve(s)
         for e in range(depths):
             image_copy(s, lax.rem(d + e, depths)).start()
             stat_copy(s, lax.rem(d + e, depths)).start()
-        return carry
-
-    lax.fori_loop(1, groups, serve_other, 0, unroll=True)
 
     remote(states_recv.at[pl.ds(0, mps - 1)], states_recv.at[pl.ds(0, mps - 1)], state_ssem, state_rsem, g, d, m).wait_recv()
     smalls[9].wait()
@@ -491,10 +495,13 @@
     def proj_copy(k, peer):
         return remote(proj_send.at[k], proj_recv.at[m], proj_ssem, proj_rsem, g, d, peer)
 
+    ahead = project(far[0])
     for k, peer in enumerate(far):
-        proj_send[k] = project(peer).astype(BF16)
+        block = ahead
+        ahead = project((far + [m])[k + 1])
+        proj_send[k] = block.astype(BF16)
         proj_copy(k, peer).start()
-    total = project(m) + states_rows[...]
+    total = ahead + states_rows[...]
     sent = proj_send.at[pl.ds(0, mps - 1)]
     remote(sent, proj_recv.at[pl.ds(0, mps - 1)], proj_ssem, proj_rsem, g, d, m).wait_recv()
     for k in range(1, mps):
@@ -506,23 +513,42 @@
     square_lane = lax.broadcasted_iota(I32, (per_depth, width), 1)
     square_row = lax.broadcasted_iota(I32, (per_depth, width), 0)
     diagonal = square_lane == square_row
-    square_all[me] = jnp.sum(jnp.where(diagonal, square, 0.0), axis=0, keepdims=True)
+    square_cols[m] = jnp.sum(jnp.where(diagonal, square, 0.0), axis=0, keepdims=True)
 
     pl.semaphore_wait(ready_sem, mps - 1)
 
     def x_copy(gg, mm):
         return remote(x_all.at[me], x_all.at[me], x_ssem, x_rsem.at[m], gg, d, mm)
 
-    def square_copy(gg, mm):
-        return remote(square_all.at[me], square_all.at[me], square_ssem, square_rsem, gg, d, mm)
-
-    targets = [(peer, m) for peer in plane]
-    for block in far:
-        targets += [((g + k) % groups, block) for k in range(groups)]
-    for gg, mm in targets:
-        x_copy(gg, mm).start()
-    for gg, mm in targets:
-        square_copy(gg, mm).start()
+    def column_copy(peer):
+        return remote(
+            square_cols.at[m], square_cols.at[m], square_ssem.at[0], square_rsem.at[0], g, d, peer
+        )
+
+    def square_copy(peer):
+        return remote(
+            square_all.at[g], square_all.at[g], square_ssem.at[1], square_rsem.at[1], peer, d, m
+        )
+
+    ring = [lax.rem(g * mps + m + k, pieces) for k in range(1, pieces)]
+    targets = [(lax.div(p, mps), lax.rem(p, mps)) for p in ring]
+    relayed = lax.rem(m + mps // 2, mps)
+    handed = relayed * groups + g
+
+    def hand_copy():
+        return remote(x_all.at[me], x_all.at[me], x_ssem, hand_rsem, g, d, relayed)
+
+    def pass_copy(peer):
+        return remote(
+            x_all.at[handed], x_all.at[handed], x_ssem, x_rsem.at[relayed], peer, d, m
+        )
+
+    hand_copy().start()
+    for peer in far:
+        column_copy(peer).start()
+    for k, (gg, mm) in enumerate(targets):
+        if (k + 1) % mps != mps // 2:
+            x_copy(gg, mm).start()
 
     for i in range(mps):
         res_send[i] = res_cols[i * rows : (i + 1) * rows, :]
@@ -530,9 +556,6 @@
     def res_copy(peer):
         return remote(res_send.at[peer], res_recv.at[m], res_ssem, res_rsem, g, d, peer)
 
-    for peer in far:
-        res_copy(peer).start()
-    res_recv[m] = res_send[m]
 
     loads[5].wait()
     loads[6].wait()
@@ -555,21 +578,33 @@
         got = x_all.at[pl.ds(0, count)]
         remote(got, got, x_ssem, x_rsem.at[block], g, d, m).wait_recv()
 
+    remote(x_all.at[0], x_all.at[0], x_ssem, hand_rsem, g, d, m).wait_recv()
+    for peer in plane:
+        pass_copy(peer).start()
+    got = square_cols.at[pl.ds(0, mps - 1)]
+    remote(got, got, square_ssem.at[0], square_rsem.at[0], g, d, m).wait_recv()
+    square_all[g] = sum(square_cols[i] for i in range(mps))
+    for peer in plane:
+        square_copy(peer).start()
+
     x_wait(m, groups - 1)
     expand(m, True)
-    for i, block in enumerate([lax.rem(m + k, mps) for k in range(1, mps)]):
-        if i == mps - 2:
-            got = square_all.at[pl.ds(0, pieces - 1)]
-            remote(got, got, square_ssem, square_rsem, g, d, m).wait_recv()
-            scales = []
-            for s in range(groups):
-                row = sum(square_all[i2 * groups + s] for i2 in range(mps))
-                row = jnp.broadcast_to(row, (per_depth, width))
-                mean = jnp.sum(jnp.where(diagonal, row, 0.0), axis=-1, keepdims=True) / model
-                scales.append(lax.rsqrt(mean + NORM_EPSILON))
-            scale = jnp.concatenate(scales, axis=0)
+    for block in near:
         x_wait(block, groups)
         expand(block, False)
+    got = square_all.at[pl.ds(0, groups - 1)]
+    remote(got, got, square_ssem.at[1], square_rsem.at[1], g, d, m).wait_recv()
+    scales = []
+    for s in range(groups):
+        row = jnp.broadcast_to(square_all[s], (per_depth, width))
+        mean = jnp.sum(jnp.where(diagonal, row, 0.0), axis=-1, keepdims=True) / model
+        scales.append(lax.rsqrt(mean + NORM_EPSILON))
+    scale = jnp.concatenate(scales, axis=0)
+    x_wait(relayed, groups - 1)
+    expand(relayed, False)
+    for peer in far:
+        res_copy(peer).start()
+    res_recv[m] = res_send[m]
     v = gate_sum[...] * scale
     hidden[...] = (v / (1.0 + jnp.exp(-v)) * (up_sum[...] * scale)).astype(BF16)
 
@@ -584,7 +619,6 @@
             mm,
         )
 
-    order = targets[groups - 1 :] + targets[: groups - 1]
     for n in range(chunks):
         columns = slice(n * part_cols, (n + 1) * part_cols)
         part = jnp.dot(hidden[...], down[:, columns], preferred_element_type=F32)
@@ -592,7 +626,7 @@
             for i in range(mps):
                 at = s * per_depth + i * rows
                 down_send[n, i * groups + s] = part[at : at + rows, :].astype(BF16)
-        for gg, mm in order:
+        for gg, mm in targets:
             down_copy(n, gg, mm).start()
     down_recv[me] = down_send[:, me]
 
@@ -626,7 +660,8 @@
     sent_all(stat_all, stat_ssem, stat_rsem)
     sent_all(proj_send.at[pl.ds(0, mps - 1)], proj_ssem, proj_rsem)
     sent_all(x_all.at[pl.ds(0, pieces - 1)], x_ssem, x_rsem.at[0])
-    sent_all(square_all.at[pl.ds(0, pieces - 1)], square_ssem, square_rsem)
+    sent_all(square_cols.at[pl.ds(0, mps - 1)], square_ssem.at[0], square_rsem.at[0])
+    sent_all(square_all.at[pl.ds(0, groups - 1)], square_ssem.at[1], square_rsem.at[1])
     sent_all(res_send.at[pl.ds(0, mps - 1)], res_ssem, res_rsem)
     sent_all(down_recv.at[pl.ds(0, pieces - 1)], down_ssem, down_rsem)
 
@@ -724,7 +759,8 @@
         pltpu.VMEM((mps, rows, cols), F32),
         pltpu.VMEM((mps, rows, cols), F32),
         pltpu.VMEM((pieces, per_depth, cols), BF16),
-        pltpu.VMEM((pieces, 1, width), F32),
+        pltpu.VMEM((mps, 1, width), F32),
+        pltpu.VMEM((groups, 1, width), F32),
         pltpu.VMEM((groups * per_depth, units), F32),
         pltpu.VMEM((groups * per_depth, units), F32),
         pltpu.VMEM((groups * per_depth, units), BF16),
@@ -747,7 +783,8 @@
         dma,
         dma((mps,)),
         dma,
-        dma,
+        dma((2,)),
+        dma((2,)),
         dma,
         dma,
         dma,

time: 37.5 us -> 34.4 us (0.917)
  Pallas kernels: 36.7 us -> 33.6 us
    pallas_call x1, Pallas kernels: 36.1 us -> 32.9 us  [on_device(): pl.pallas_call(functools.partial(kernel, (groups, depths, mps)), out_shap...]
where the time goes in v2:
time: 34.4 us; the launch traced here: 34.2 us
  Pallas kernels  33.6 us (98%)
  between operations  0.65 us (2%)
    pallas_call x1, Pallas kernels, on_device(): pl.pallas_call(functools.partial(kernel, (groups, depths, mps)), out_shap...  32.9 us

profile of v2, /device:TPU:0, one launch (start us, length us, event | category | flops | bytes accessed | tf_op | source)
XLA Modules:
  0.0 34.2 jit_solution(17850962074922203188)
XLA Ops:
  0.6 32.9 %shard_map.194 = (bf16[8,8,128]{2,1,0:T(8,128)(2,1)S(1)}, bf16[2,4096]{1,0:T(2,128)(2,1)S(1)}) custom-call(bf16[2,4096]{1,0:T(2,128)(2,1)} %states_hbm.1, bf16[16,8,128]{2,1,0:T(8,128)(2,1)} %queries_hbm.1, bf16[16,2,128]{2,1,0:T(2,128)(2,1)} %new_keys_hbm.1, bf16[16,2,128]{2,1,0:T(2,128)(2,1)} %new_values_hbm.1, f32[1,4096]{1,0:T(1,128)} %bitcast.1, ...), custom_call_target="tpu_custom_call" | custom-call | tf_op jit(solution)/shard_map/pallas_call | solution.py:794
  33.6 0.6 %shard_map.195 = (bf16[8,8,128]{2,1,0:T(8,128)(2,1)}, bf16[2,4096]{1,0:T(2,128)(2,1)}) custom-call(bf16[8,8,128]{2,1,0:T(8,128)(2,1)S(1)} %get-tuple-element.4.attention, bf16[2,4096]{1,0:T(2,128)(2,1)S(1)} %get-tuple-element.5.layer), custom_call_target="tpu_custom_call" | custom-call | tf_op jit(solution)/shard_map/pallas_call | solution.py:807

commit v3 on v2

--- a/solution.py
+++ b/solution.py
@@ -84,8 +84,7 @@
     res_send,
     res_recv,
     x_all,
-    square_cols,
-    square_all,
+    square_sum,
     gate_sum,
     up_sum,
     hidden,
@@ -108,8 +107,6 @@
     x_ssem,
     x_rsem,
     hand_rsem,
-    square_ssem,
-    square_rsem,
     res_ssem,
     res_rsem,
     down_ssem,
@@ -176,7 +173,7 @@
         (queries_hbm, queries),
         (new_keys_hbm, new_keys),
         (new_values_hbm, new_values),
-        (gain_hbm.at[:, own_columns], gain),
+        (gain_hbm, gain),
         (states_hbm.at[:, own_columns], states_recv.at[m]),
     )
     smalls = [pltpu.make_async_copy(a, b, small_sem.at[i]) for i, (a, b) in enumerate(small_pairs)]
@@ -508,27 +505,12 @@
         total = total + proj_recv[lax.rem(m + k, mps)].astype(F32)
     res_cols[...] = total
     me = m * groups + g
-    x_all[me] = (total * gain[...]).astype(BF16)
-    square = jnp.broadcast_to(jnp.sum(total * total, axis=-1, keepdims=True), (per_depth, width))
-    square_lane = lax.broadcasted_iota(I32, (per_depth, width), 1)
-    square_row = lax.broadcasted_iota(I32, (per_depth, width), 0)
-    diagonal = square_lane == square_row
-    square_cols[m] = jnp.sum(jnp.where(diagonal, square, 0.0), axis=0, keepdims=True)
+    x_all[me] = (total * gain[:, own_columns]).astype(BF16)
 
     pl.semaphore_wait(ready_sem, mps - 1)
 
     def x_copy(gg, mm):
         return remote(x_all.at[me], x_all.at[me], x_ssem, x_rsem.at[m], gg, d, mm)
-
-    def column_copy(peer):
-        return remote(
-            square_cols.at[m], square_cols.at[m], square_ssem.at[0], square_rsem.at[0], g, d, peer
-        )
-
-    def square_copy(peer):
-        return remote(
-            square_all.at[g], square_all.at[g], square_ssem.at[1], square_rsem.at[1], peer, d, m
-        )
 
     ring = [lax.rem(g * mps + m + k, pieces) for k in range(1, pieces)]
     targets = [(lax.div(p, mps), lax.rem(p, mps)) for p in ring]
@@ -544,8 +526,6 @@
         )
 
     hand_copy().start()
-    for peer in far:
-        column_copy(peer).start()
     for k, (gg, mm) in enumerate(targets):
         if (k + 1) % mps != mps // 2:
             x_copy(gg, mm).start()
@@ -563,16 +543,23 @@
 
     def expand(block, first):
         tokens = [x_all[block * groups + s].astype(F32) for s in range(groups)]
-        tokens = jnp.concatenate(tokens, axis=0).astype(BF16)
+        tokens = jnp.concatenate(tokens, axis=0)
         part = pl.ds(pl.multiple_of(block * cols, cols), cols)
+        plain = tokens * (1.0 / gain[:, part])
+        squares = sum(
+            plain[:, i : i + width] * plain[:, i : i + width] for i in range(0, cols, width)
+        )
+        tokens = tokens.astype(BF16)
         a = jnp.dot(tokens, gate[part, :], preferred_element_type=F32)
         b = jnp.dot(tokens, up[part, :], preferred_element_type=F32)
         if first:
             gate_sum[...] = a
             up_sum[...] = b
+            square_sum[...] = squares
         else:
             gate_sum[...] += a
             up_sum[...] += b
+            square_sum[...] += squares
 
     def x_wait(block, count):
         got = x_all.at[pl.ds(0, count)]
@@ -581,30 +568,18 @@
     remote(x_all.at[0], x_all.at[0], x_ssem, hand_rsem, g, d, m).wait_recv()
     for peer in plane:
         pass_copy(peer).start()
-    got = square_cols.at[pl.ds(0, mps - 1)]
-    remote(got, got, square_ssem.at[0], square_rsem.at[0], g, d, m).wait_recv()
-    square_all[g] = sum(square_cols[i] for i in range(mps))
-    for peer in plane:
-        square_copy(peer).start()
-
     x_wait(m, groups - 1)
     expand(m, True)
     for block in near:
         x_wait(block, groups)
         expand(block, False)
-    got = square_all.at[pl.ds(0, groups - 1)]
-    remote(got, got, square_ssem.at[1], square_rsem.at[1], g, d, m).wait_recv()
-    scales = []
-    for s in range(groups):
-        row = jnp.broadcast_to(square_all[s], (per_depth, width))
-        mean = jnp.sum(jnp.where(diagonal, row, 0.0), axis=-1, keepdims=True) / model
-        scales.append(lax.rsqrt(mean + NORM_EPSILON))
-    scale = jnp.concatenate(scales, axis=0)
     x_wait(relayed, groups - 1)
     expand(relayed, False)
     for peer in far:
         res_copy(peer).start()
     res_recv[m] = res_send[m]
+    spread = jnp.sum(square_sum[...], axis=-1, keepdims=True) / model
+    scale = lax.rsqrt(spread + NORM_EPSILON)
     v = gate_sum[...] * scale
     hidden[...] = (v / (1.0 + jnp.exp(-v)) * (up_sum[...] * scale)).astype(BF16)
 
@@ -626,8 +601,10 @@
             for i in range(mps):
                 at = s * per_depth + i * rows
                 down_send[n, i * groups + s] = part[at : at + rows, :].astype(BF16)
-        for gg, mm in targets:
-            down_copy(n, gg, mm).start()
+        for shift in [mps // 2] + [k for k in range(mps) if k != mps // 2]:
+            for k, (gg, mm) in enumerate(targets):
+                if (k + 1) % mps == shift:
+                    down_copy(n, gg, mm).start()
     down_recv[me] = down_send[:, me]
 
     got = res_recv.at[pl.ds(0, mps - 1)]
@@ -660,8 +637,6 @@
     sent_all(stat_all, stat_ssem, stat_rsem)
     sent_all(proj_send.at[pl.ds(0, mps - 1)], proj_ssem, proj_rsem)
     sent_all(x_all.at[pl.ds(0, pieces - 1)], x_ssem, x_rsem.at[0])
-    sent_all(square_cols.at[pl.ds(0, mps - 1)], square_ssem.at[0], square_rsem.at[0])
-    sent_all(square_all.at[pl.ds(0, groups - 1)], square_ssem.at[1], square_rsem.at[1])
     sent_all(res_send.at[pl.ds(0, mps - 1)], res_ssem, res_rsem)
     sent_all(down_recv.at[pl.ds(0, pieces - 1)], down_ssem, down_rsem)
 
@@ -732,7 +707,7 @@
         down_weight,
     )
     scratch = [pltpu.VMEM(a.shape, a.dtype) for a in small[1:4]]
-    scratch += [pltpu.VMEM((1, cols), norm_gain.dtype)]
+    scratch += [pltpu.VMEM((1, model), norm_gain.dtype)]
     scratch += [pltpu.SMEM(a.shape, a.dtype) for a in small[5:]]
     scratch += [pltpu.VMEM(a.shape, a.dtype) for a in big]
     scratch += [
@@ -759,8 +734,7 @@
         pltpu.VMEM((mps, rows, cols), F32),
         pltpu.VMEM((mps, rows, cols), F32),
         pltpu.VMEM((pieces, per_depth, cols), BF16),
-        pltpu.VMEM((mps, 1, width), F32),
-        pltpu.VMEM((groups, 1, width), F32),
+        pltpu.VMEM((groups * per_depth, width), F32),
         pltpu.VMEM((groups * per_depth, units), F32),
         pltpu.VMEM((groups * per_depth, units), F32),
         pltpu.VMEM((groups * per_depth, units), BF16),
@@ -783,8 +757,6 @@
         dma,
         dma((mps,)),
         dma,
-        dma((2,)),
-        dma((2,)),
         dma,
         dma,
         dma,

time: 34.4 us -> 34 us (0.988)
  Pallas kernels: 33.6 us -> 33.2 us
    pallas_call x1, Pallas kernels: 32.9 us -> 32.6 us  [on_device(): pl.pallas_call(functools.partial(kernel, (groups, depths, mps)), out_shap...]
where the time goes in v3:
time: 34 us; the launch traced here: 33.8 us
  Pallas kernels  33.2 us (98%)
  between operations  0.65 us (2%)
    pallas_call x1, Pallas kernels, on_device(): pl.pallas_call(functools.partial(kernel, (groups, depths, mps)), out_shap...  32.6 us

profile of v3, /device:TPU:0, one launch (start us, length us, event | category | flops | bytes accessed | tf_op | source)
XLA Modules:
  0.0 33.8 jit_solution(15451920116551842785)
XLA Ops:
  0.6 32.6 %shard_map.194 = (bf16[8,8,128]{2,1,0:T(8,128)(2,1)S(1)}, bf16[2,4096]{1,0:T(2,128)(2,1)S(1)}) custom-call(bf16[2,4096]{1,0:T(2,128)(2,1)} %states_hbm.1, bf16[16,8,128]{2,1,0:T(8,128)(2,1)} %queries_hbm.1, bf16[16,2,128]{2,1,0:T(2,128)(2,1)} %new_keys_hbm.1, bf16[16,2,128]{2,1,0:T(2,128)(2,1)} %new_values_hbm.1, f32[1,4096]{1,0:T(1,128)} %bitcast.1, ...), custom_call_target="tpu_custom_call" | custom-call | tf_op jit(solution)/shard_map/pallas_call | solution.py:766
  33.2 0.6 %shard_map.195 = (bf16[8,8,128]{2,1,0:T(8,128)(2,1)}, bf16[2,4096]{1,0:T(2,128)(2,1)}) custom-call(bf16[8,8,128]{2,1,0:T(8,128)(2,1)S(1)} %get-tuple-element.4.attention, bf16[2,4096]{1,0:T(2,128)(2,1)S(1)} %get-tuple-element.5.layer), custom_call_target="tpu_custom_call" | custom-call | tf_op jit(solution)/shard_map/pallas_call | solution.py:779
